TPU v7x, 8 devices: a whole 2x2x1 slice. The times are simulated.
8 devices in a mesh: data: 1 (over z), col: 2 (over y), row: 4 (over x, core).
Axes of the slice: x: 2, y: 2, z: 1, core: 2. Of those that a mesh axis runs over, the one named last changes fastest.
Arguments:
- image: bfloat16 [256, 128, 3], P(('data', 'row'), 'col')
- w_enc1a: bfloat16 [3, 3, 3, 192], replicated
- b_enc1a: float32 [192], replicated
- w_enc1b: bfloat16 [3, 3, 192, 192], replicated
- b_enc1b: float32 [192], replicated
- w_enc2a: bfloat16 [3, 3, 192, 384], replicated
- b_enc2a: float32 [384], replicated
- w_enc2b: bfloat16 [3, 3, 384, 384], replicated
- b_enc2b: float32 [384], replicated
- w_mid_a: bfloat16 [3, 3, 384, 768], replicated
- b_mid_a: float32 [768], replicated
- w_mid_b: bfloat16 [3, 3, 768, 768], replicated
- b_mid_b: float32 [768], replicated
- w_up2: bfloat16 [2, 2, 768, 384], replicated
- w_dec2a: bfloat16 [3, 3, 768, 384], replicated
- b_dec2a: float32 [384], replicated
- w_dec2b: bfloat16 [3, 3, 384, 384], replicated
- b_dec2b: float32 [384], replicated
- w_up1: bfloat16 [2, 2, 384, 192], replicated
- w_dec1a: bfloat16 [3, 3, 384, 192], replicated
- b_dec1a: float32 [192], replicated
- w_dec1b: bfloat16 [3, 3, 192, 192], replicated
- b_dec1b: float32 [192], replicated
- w_head: bfloat16 [192, 6], replicated
- b_head: float32 [6], replicated
Outputs:
- output: float32 [256, 128, 6], P(('data', 'row'), 'col')
All inputs are finite; a program needn't handle non-finite values.
Results may differ from a plain program's by a relative error of at most 0.0168.
Values are sent between devices in bfloat16 or wider.
A program may use at most 1 GiB of HBM per device.

v0:
```python
import functools

import jax
import jax.numpy as jnp
from jax import lax
from jax.experimental import pallas as pl
from jax.experimental.pallas import tpu as pltpu
from jax.sharding import PartitionSpec as P

MESH = pl.DeviceIdType.MESH
F32 = jnp.float32
BF16 = jnp.bfloat16
ROWS = 18
SIDE = 16
PIX = SIDE * SIDE
EXT = ROWS * SIDE
C1 = 192
C1P = 256
C2 = 384
C3 = 768
HALF = 64
LANE = 128
PATCH = 192
TAPROWS = 40
BY_ROWS = (((1,), (1,)), ((), ()))
POOL1, ENC2A, POOL2, MIDA, UP2, DEC2A, CAT1, DEC1A, IMAGE, SKIP2 = range(10)
EXCHANGE = ((2, C1P), (2, C2), (1, C2), (1, C3), (2, C2), (2, C2), (4, C2), (4, C1P), (1, LANE), (2, C2))
MESSAGES = 5
LOADS = 19


def iota(shape, dim):
    return lax.broadcasted_iota(jnp.int32, shape, dim)


def grid_iota(*shape):
    return iota(shape, 0), iota(shape, 1)


def ones_at(mask):
    return mask.astype(F32).astype(BF16)


def dot(lhs, rhs):
    return jnp.dot(lhs, rhs, preferred_element_type=F32)


def dot_rows(lhs, rhs):
    return lax.dot_general(lhs, rhs, BY_ROWS, preferred_element_type=F32)


def biased_relu(acc, bias):
    return jnp.maximum(acc + bias[...].reshape(1, bias.shape[-1]), 0.0).astype(BF16)


def kernel(row_count, x, we1a, we1b, we2a, we2b, wma, wmb, wu2, wd2a, wd2b, wu1, wd1a, wd1b, wh,
           be1a, be1b, be2a, be2b, bma, bmb, bd2a, bd2b, bd1a, bd1b, bh, y, *scratch):
    (vw8, re1b, ve1b, ve2a, ve2b, vma, vmb, vu2, vd2a, vu1, vd1a, vd1b,
     h1, cat1, d1a, p1, e2a, cat2, d2, p2, ma, mid, x1, x8, wf, bpad, weave, part) = scratch[:-2 * len(EXCHANGE) - 3]
    send_cols = scratch[-2 * len(EXCHANGE) - 3:-len(EXCHANGE) - 3]
    recv_cols = scratch[-len(EXCHANGE) - 3:-3]
    w_sem, send_sem, recv_sem = scratch[-3:]
    row, col, data = lax.axis_index("row"), lax.axis_index("col"), lax.axis_index("data")
    last = row_count - 1
    has_up, has_down = row > 0, row < last
    up, down = (data, col, row - 1), (data, col, row + 1)
    side, side_up, side_down = (data, 1 - col, row), (data, 1 - col, row - 1), (data, 1 - col, row + 1)
    edge = (1 - col) * (SIDE - 1)

    loads = [(we1b, re1b), (we2a, ve2a.at[:, :, HALF:, :]), (we2b, ve2b), (wma, vma), (wmb, vmb),
             (wu2, vu2), (wd2a, vd2a), (wu1, vu1)]
    loads += [(wd1a.at[t // 3, t % 3], vd1a.at[:C1, pl.ds(t * C2, C2)]) for t in range(9)]
    loads += [(wd1b, vd1b.at[:, :, :C1, :]), (wd2b, ve2b)]
    copies = [pltpu.make_async_copy(src, dst, w_sem.at[k]) for k, (src, dst) in enumerate(loads)]
    for copy in copies[:3]:
        copy.start()
    for buf, factor in ((h1, 4), (cat1, 4), (d1a, 4), (p1, 2), (e2a, 2), (cat2, 2), (p2, 1), (ma, 1), (x1, 1)):
        blank = jnp.zeros(buf.shape[1:2] + buf.shape[3:], BF16)
        buf[0, :, ROWS - 1] = blank
        buf[factor - 1, :, 0] = blank
    for buf, (factor, _) in zip(recv_cols, EXCHANGE):
        buf[factor:] = jnp.zeros((2,) + buf.shape[1:], BF16)

    barrier = pltpu.get_barrier_semaphore()

    def arrive(device):
        pl.semaphore_signal(barrier, inc=1, device_id=device, device_id_type=MESH)

    arrive(side)

    @pl.when(has_up)
    def _():
        arrive(up)
        arrive(side_up)

    @pl.when(has_down)
    def _():
        arrive(down)
        arrive(side_down)

    for copy in copies[3:-1]:
        copy.start()

    def messages(index, buf, lane):
        factor, width = EXCHANGE[index]
        cols, got = send_cols[index], recv_cols[index]
        own = pl.ds(1, factor)
        lanes = pl.ds(lane, width)

        def remote(k, src, dst, device):
            return pltpu.make_async_remote_copy(
                src_ref=src, dst_ref=dst, send_sem=send_sem.at[index, k], recv_sem=recv_sem.at[index, k],
                device_id=device, device_id_type=MESH)

        routes = (
            (cols, got.at[pl.ds(0, factor)], side),
            (buf.at[0, own, 1, :, lanes], buf.at[0, own, ROWS - 1, :, lanes], up),
            (buf.at[factor - 1, own, ROWS - 2, :, lanes], buf.at[factor - 1, own, 0, :, lanes], down),
            (cols.at[0], got.at[factor + 1], side_up),
            (cols.at[factor - 1], got.at[factor], side_down),
        )
        return [remote(k, *route) for k, route in enumerate(routes)]

    def shift(value, right):
        value = value.astype(F32)
        count = value.shape[0]
        at = lax.rem(iota(value.shape, 0), SIDE)
        if right:
            return jnp.where(at == SIDE - 1, 0.0, pltpu.roll(value, count - 1, 0))
        return jnp.where(at == 0, 0.0, pltpu.roll(value, 1, 0))

    def start(index, buf, lane=0):
        factor, width = EXCHANGE[index]
        lanes = pl.ds(lane, width)
        to_side, to_up, to_down, to_side_up, to_side_down = messages(index, buf, lane)
        if index == IMAGE:
            pl.semaphore_wait(barrier, 2 * has_up.astype(jnp.int32) + 2 * has_down.astype(jnp.int32) + 1)

        @pl.when(has_up)
        def _():
            to_up.start()

        @pl.when(has_down)
        def _():
            to_down.start()

        pick_row, pick_at = grid_iota(SIDE, PIX)
        pick = ones_at(pick_at == pick_row * SIDE + edge)
        cols = send_cols[index]
        for a in range(factor):
            plane = buf[a, 1 + (factor - 1) * (1 - col), 1:ROWS - 1, :, lanes].reshape(PIX, width)
            cols[a] = dot(pick, plane).astype(BF16)
        to_side.start()

        @pl.when(has_up)
        def _():
            to_side_up.start()

        @pl.when(has_down)
        def _():
            to_side_down.start()

        def shifted(a):
            for source, target in ((factor, 0), (1, factor + 1)):
                value = shift(buf[a, source, 1:ROWS - 1, :, lanes].reshape(PIX, width), target > 0)
                buf[a, target, 1:ROWS - 1, :, lanes] = value.astype(BF16).reshape(SIDE, SIDE, width)

        if factor == 1:
            shifted(0)
        else:
            pl.loop(0, factor)(shifted)

    def finish(index, buf, lane=0):
        factor, width = EXCHANGE[index]
        lanes = pl.ds(lane, width)
        got = recv_cols[index]
        to_side, to_up, to_down, to_side_up, to_side_down = messages(index, buf, lane)
        to_side.wait()

        @pl.when(has_up)
        def _():
            to_up.wait_send()
            to_side_up.wait_send()
            to_down.wait_recv()
            to_side_down.wait_recv()

        @pl.when(has_down)
        def _():
            to_down.wait_send()
            to_side_down.wait_send()
            to_up.wait_recv()
            to_side_up.wait_recv()

        at, source = grid_iota(EXT, 3 * SIDE)
        place = ones_at((lax.rem(at, SIDE) == edge) & (at // SIDE + SIDE - 1 == source))
        fix = (factor + 1) * (1 - col)
        for a in range(factor):
            put = dot(place, jnp.concatenate([got[factor], got[a], got[factor + 1]], axis=0))
            plane = buf[a, fix, 1:ROWS - 1, :, lanes].reshape(PIX, width).astype(F32) + put[SIDE:EXT - SIDE]
            buf[a, fix, 1:ROWS - 1, :, lanes] = plane.astype(BF16).reshape(SIDE, SIDE, width)
            ends = ([(0, put[:SIDE])] if a == factor - 1 else []) + ([(ROWS - 1, put[EXT - SIDE:])] if a == 0 else [])
            for line, corner in ends:
                left = shift(buf[a, factor, line, :, lanes], False) + jnp.where(col == 1, corner, 0.0)
                right = shift(buf[a, 1, line, :, lanes], True) + jnp.where(col == 0, corner, 0.0)
                buf[a, 0, line, :, lanes] = left.astype(BF16)
                buf[a, factor + 1, line, :, lanes] = right.astype(BF16)

    ALL = [(dy, dx) for dy in range(3) for dx in range(3)]

    def gather(buf, factor, a, bs, taps, lane=0, width=None):
        lanes = pl.ds(lane, buf.shape[-1] if width is None else width)
        rows = []
        for b in bs:
            parts = []
            for dy, dx in taps:
                shifted = a + (dy - 1 + factor)
                piece = buf[lax.rem(shifted, factor), b + dx, pl.ds(shifted // factor, SIDE), :, lanes]
                parts.append(piece.reshape(PIX, piece.shape[-1]))
            rows.append(jnp.concatenate(parts, axis=1))
        return jnp.concatenate(rows, axis=0)

    def conv(buf, factor, a, bs, weight):
        return dot(gather(buf, factor, a, bs, ALL), weight[...].reshape(9 * buf.shape[-1], weight.shape[-1]))

    def put_planes(buf, a, bs, value, lane=0):
        width = value.shape[-1]
        for k, b in enumerate(bs):
            plane = value[k * PIX:(k + 1) * PIX].reshape(SIDE, SIDE, width)
            buf[a, b + 1, 1:ROWS - 1, :, lane:lane + width] = plane

    def pool(src, dst, factor, lane, width):
        for a in range(factor):
            for b in range(factor):
                quad = [src[2 * a + p, 2 * b + q + 1, 1:ROWS - 1, :, lane:lane + width] for p in range(2) for q in range(2)]
                dst[a, b + 1, 1:ROWS - 1] = functools.reduce(jnp.maximum, quad)

    LEVEL2 = [(a, b) for a in range(2) for b in range(2)]

    def near(a, b):
        return [(dy, dx) for dy, dx in ALL if dy != 2 * a and dx != 2 * b]

    def weights_of(weight, taps):
        return jnp.concatenate([weight[dy, dx] for dy, dx in taps], axis=0)

    def conv_level2(index, src, weight, bias, put):
        start(index, src)
        for a, b in LEVEL2:
            taps = near(a, b)
            part[2 * a + b] = dot(gather(src, 2, a, (b,), taps), weights_of(weight, taps))
        finish(index, src)
        for a, b in LEVEL2:
            taps = [tap for tap in ALL if tap not in near(a, b)]
            acc = part[2 * a + b] + dot(gather(src, 2, a, (b,), taps), weights_of(weight, taps))
            put(a, b, biased_relu(acc, bias))

    at, to = grid_iota(HALF, HALF)
    split_cols = ones_at(at == lax.rem(to, SIDE) * 4 + to // SIDE)
    at, to = grid_iota(PIX, HALF)
    own_col = lax.rem(at, SIDE) == lax.rem(to, SIDE)
    fold_at, fold_to = grid_iota(HALF, LANE)
    image = []
    for ch in range(3):
        cols = dot(x[ch], split_cols).astype(BF16)
        for a in range(4):
            spread = ones_at(to == (at // SIDE) * 4 + a)
            lines = jnp.where(own_col, dot(spread, cols), 0.0).astype(BF16)
            image.append(dot(lines, ones_at(fold_to == fold_at // SIDE + (ch * SIDE + a * 4))))
    x1[0, 1, 1:ROWS - 1] = sum(image[1:], image[0]).astype(BF16).reshape(SIDE, SIDE, LANE)
    start(IMAGE, x1)

    wf[...] = jnp.zeros(wf.shape, F32)
    for t in range(9):
        wf[pl.ds(4 * t, 3), :C1] = we1a[t // 3, t % 3].astype(F32)
    k, m = grid_iota(PATCH, TAPROWS)
    py, px = k // 32, lax.rem(k, 32) // 4
    base = py * 12 + px * 4 + lax.rem(k, 4)

    @pl.loop(0, 4)
    def _(a):
        for b in range(6):
            good = (py >= a) & (py <= a + 2) & (px >= b) & (px <= b + 2)
            place = ones_at(good & (m == base - a * 12 - b * 4))
            vw8[a * 6 + b] = dot(place, wf[...].astype(BF16)).astype(BF16)

    pad = jnp.zeros((1, HALF), F32)
    bpad[0:1, :] = jnp.concatenate([be1a[...].reshape(1, C1), pad], axis=1)
    bpad[1:2, :] = jnp.concatenate([pad, be1b[...].reshape(1, C1)], axis=1)
    bpad[2:3, :] = jnp.concatenate([bd1a[...].reshape(1, C1), pad], axis=1)
    n, m = grid_iota(PIX, PIX)
    weave[...] = ones_at(m == lax.rem(n, 4) * HALF + (n // HALF) * SIDE + lax.rem(n, HALF) // 4)
    ve2a[:, :, :HALF, :] = jnp.zeros((3, 3, HALF, C2), BF16)
    vd1b[:, :, C1:, :] = jnp.zeros((3, 3, HALF, C1), BF16)
    vd1a[C1:, :] = jnp.zeros((HALF, vd1a.shape[1]), BF16)
    copies[0].wait()

    @pl.loop(0, 3)
    def _(dy):
        for dx in range(3):
            value = jnp.concatenate([jnp.zeros((C1, HALF), F32), re1b[dy, dx].astype(F32)], axis=1)
            ve1b[dy, dx, :C1] = value.astype(BF16)
            ve1b[dy, dx, C1:] = jnp.zeros((HALF, C1P), BF16)

    finish(IMAGE, x1)

    blank = jnp.zeros((SIDE, LANE), BF16)
    lane, k = grid_iota(LANE, PATCH)
    ch, a, b = lane // SIDE, lax.rem(lane, SIDE) // 4, lax.rem(lane, 4)
    patches = []
    for dx in range(3):
        plane = x1[0, dx].reshape(EXT, LANE)
        blocks = (jnp.concatenate([blank, plane[:-SIDE]], axis=0), plane, jnp.concatenate([plane[SIDE:], blank], axis=0))
        for dy, block in enumerate(blocks):
            py, px = a + (4 * dy - 3), b + (4 * dx - 2)
            good = (ch < 3) & (py >= 0) & (py < 6) & (px >= 0) & (px < 8)
            patches.append(dot(block, ones_at(good & (k == py * 32 + px * 4 + ch))))
    x8[...] = sum(patches[1:], patches[0]).astype(BF16)

    pos = iota((EXT, C1P), 0)
    pos_row, pos_col = pos // SIDE, lax.rem(pos, SIDE)
    off_rows = ((pos_row == 0) & (row == 0)) | ((pos_row == ROWS - 1) & (row == last))
    off = {0: off_rows | ((pos_col == 0) & (col == 0)), 5: off_rows | ((pos_col == SIDE - 1) & (col == 1))}

    @pl.loop(0, 4)
    def _(a):
        for b in range(6):
            acc = dot(x8[...], vw8[a * 6 + b])
            out = jnp.where(off.get(b, off_rows), 0.0, jnp.maximum(acc + bpad[0:1, :], 0.0))
            h1[a, b] = out.astype(BF16).reshape(ROWS, SIDE, C1P)

    @pl.loop(0, 4)
    def _(a):
        put_planes(cat1, a, range(4), biased_relu(conv(h1, 4, a, range(4), ve1b), bpad.at[1:2]), LANE)

    pool(cat1, p1, 2, LANE, C1P)

    copies[1].wait()
    conv_level2(POOL1, p1, ve2a, be2a, lambda a, b, value: put_planes(e2a, a, (b,), value))
    copies[2].wait()
    conv_level2(ENC2A, e2a, ve2b, be2b, lambda a, b, value: put_planes(cat2, a, (b,), value, C2))
    copies[-1].start()
    pool(cat2, p2, 1, C2, C2)

    start(POOL2, p2)
    start(SKIP2, cat2, C2)
    copies[3].wait()
    finish(POOL2, p2)
    put_planes(ma, 0, (0,), biased_relu(conv(p2, 1, 0, (0,), vma), bma))
    start(MIDA, ma)
    copies[6].wait()
    finish(SKIP2, cat2, C2)

    def half_dec2a(a, lane):
        flat = jnp.concatenate([vd2a[dy, dx, lane:lane + C2] for dy, dx in ALL], axis=0)
        return dot(gather(cat2, 2, a, range(2), ALL, lane, C2), flat)

    part[:2] = half_dec2a(0, C2).reshape(2, PIX, C2)
    copies[4].wait()
    finish(MIDA, ma)
    mid[...] = biased_relu(conv(ma, 1, 0, (0,), vmb), bmb)
    copies[5].wait()
    for p, q in LEVEL2:
        put_planes(cat2, p, (q,), dot(mid[...], vu2[p, q]).astype(BF16))
    start(UP2, cat2)
    part[2:] = half_dec2a(1, C2).reshape(2, PIX, C2)
    finish(UP2, cat2)

    @pl.loop(0, 2)
    def _(a):
        put_planes(e2a, a, range(2), biased_relu(part[pl.ds(2 * a, 2)].reshape(2 * PIX, C2) + half_dec2a(a, 0), bd2a))

    copies[-1].wait()

    def put_d2(a, b, value):
        d2[pl.ds((2 * a + b) * PIX, PIX)] = value

    conv_level2(DEC2A, e2a, ve2b, bd2b, put_d2)
    copies[7].wait()

    @pl.loop(0, 4)
    def _(t):
        p = lax.rem(t, 2)
        lhs = d2[pl.ds((t - p) * PIX, 2 * PIX)]
        for q in range(2):
            put_planes(cat1, t, (q, q + 2), dot_rows(lhs, vu1[p, q]).astype(BF16))

    for copy in copies[8:17]:
        copy.wait()

    def level1(index, src, layer):
        start(index, src)
        pl.loop(1, 3)(lambda a: layer(a, (1, 2)))
        finish(index, src)
        pl.loop(1, 3)(lambda a: layer(a, (0, 3)))
        pl.loop(0, 2)(lambda t: layer(3 * t, range(4)))

    def dec1a(a, bs):
        put_planes(d1a, a, bs, biased_relu(dot_rows(gather(cat1, 4, a, bs, ALL), vd1a[...]), bpad.at[2:3]))

    level1(CAT1, cat1, dec1a)
    copies[17].wait()
    head_bias = jnp.zeros((6, HALF), F32)
    for c in range(6):
        head_bias = jnp.where(iota(head_bias.shape, 0) == c, bh[c], head_bias)

    def dec1b(a, bs):
        put_planes(h1, a, bs, biased_relu(conv(d1a, 4, a, bs, vd1b), bd1b))
        if 0 not in bs:
            return
        for g in range(4):
            lines = pl.ds(4 * g + 1, 4)
            picked = jnp.concatenate([h1[a, b + 1, lines, :, :C1].reshape(HALF, C1) for b in range(4)], axis=0)
            head = dot_rows(wh[...], dot(weave[...], picked).astype(BF16))
            for i in range(4):
                y[4 * (4 * g + i) + a] = head[:, i * HALF:(i + 1) * HALF] + head_bias

    level1(DEC1A, d1a, dec1b)


def solution(mesh):
    tile_spec = P(("data", "row"), "col", None)

    def device_body(image_tile, *params):
        (w_enc1a, b_enc1a, w_enc1b, b_enc1b, w_enc2a, b_enc2a, w_enc2b, b_enc2b,
         w_mid_a, b_mid_a, w_mid_b, b_mid_b, w_up2, w_dec2a, b_dec2a, w_dec2b, b_dec2b,
         w_up1, w_dec1a, b_dec1a, w_dec1b, b_dec1b, w_head, b_head) = params
        anywhere = pl.BlockSpec(memory_space=pl.ANY)
        vmem = pl.BlockSpec(memory_space=pltpu.VMEM)
        operands = [
            jnp.transpose(image_tile, (2, 0, 1)), w_enc1a, w_enc1b, w_enc2a, w_enc2b, w_mid_a, w_mid_b,
            w_up2, w_dec2a, w_dec2b, jnp.swapaxes(w_up1, 2, 3), jnp.swapaxes(w_dec1a, 2, 3), w_dec1b, w_head.T,
            b_enc1a, b_enc1b, b_enc2a, b_enc2b, b_mid_a, b_mid_b, b_dec2a, b_dec2b, b_dec1a, b_dec1b, b_head,
        ]
        specs = [vmem] * 2 + [anywhere] * 11 + [vmem] * 11 + [pl.BlockSpec(memory_space=pltpu.SMEM)]

        def kept(*shape, dtype=BF16):
            return pltpu.VMEM(shape, dtype)

        def level(factor, lanes):
            return kept(factor, factor + 2, ROWS, SIDE, lanes)

        scratch = [
            kept(24, PATCH, C1P), kept(3, 3, C1, C1), kept(3, 3, C1P, C1P), kept(3, 3, C1P, C2), kept(3, 3, C2, C2),
            kept(3, 3, C2, C3), kept(3, 3, C3, C3), kept(2, 2, C3, C2), kept(3, 3, C3, C2),
            kept(2, 2, C1, C2), kept(C1P, 9 * C2), kept(3, 3, C1P, C1),
            level(4, C1P), level(4, C2), level(4, C1P), level(2, C1P), level(2, C2), level(2, C3),
            kept(4 * PIX, C2), level(1, C2), level(1, C3), kept(PIX, C3), level(1, LANE), kept(EXT, PATCH),
            kept(TAPROWS, C1P, dtype=F32), kept(3, C1P, dtype=F32), kept(PIX, PIX),
            kept(4, PIX, C2, dtype=F32),
        ]
        scratch += [kept(factor, SIDE, width) for factor, width in EXCHANGE]
        scratch += [kept(factor + 2, SIDE, width) for factor, width in EXCHANGE]
        links = pltpu.SemaphoreType.DMA((len(EXCHANGE), MESSAGES))
        scratch += [pltpu.SemaphoreType.DMA((LOADS,)), links, links]
        out = pl.pallas_call(
            functools.partial(kernel, mesh.shape["row"]),
            name="unet",
            out_shape=jax.ShapeDtypeStruct((HALF, 6, HALF), F32),
            in_specs=specs,
            out_specs=vmem,
            scratch_shapes=scratch,
            compiler_params=pltpu.CompilerParams(collective_id=0, has_side_effects=True, vmem_limit_bytes=67043328),
        )(*operands)
        return jnp.transpose(out, (0, 2, 1))

    def program(image, *params):
        mapped = jax.shard_map(device_body, mesh=mesh, in_specs=(tile_spec,) + tuple([P()] * len(params)), out_specs=tile_spec, check_vma=False)
        return mapped(image, *params)

    return program
```

profile of v0, /device:TPU:0, one launch (start us, length us, event | category | flops | bytes accessed | tf_op | source)
XLA Modules:
  0.0 81.7 jit_solution(4551870321884770319)
XLA Ops:
  0.0 80.0 %unet.1 = f32[64,6,64]{2,1,0:T(8,128)} custom-call(bf16[3,64,64]{2,1,0:T(8,128)(2,1)} %bitcast.8, bf16[3,3,3,192]{3,2,1,0:T(4,128)(2,1)} %we1a.1, bf16[3,3,192,192]{3,2,1,0:T(8,128)(2,1)} %we1b.1, bf16[3,3,192,384]{3,2,1,0:T(8,128)(2,1)} %we2a.1, bf16[3,3,384,384]{3,2,1,0:T(8,128)(2,1)} %we2b.1, bf16[3,3,384,768]{3,2,1,0:T(8,128)(2,1)} %wma.1, ...), custom_call_target="tpu_custom_call" | custom-call | tf_op jit(solution)/shard_map/unet/pallas_call | solution.py:454
  80.0 1.7 %copy.26 = f32[64,64,6]{1,0,2:T(8,128)} copy(f32[64,64,6]{1,2,0:T(8,128)} %bitcast.6) | data formatting | bytes 196608 | tf_op jit(solution)/shard_map/transpose | solution.py:463
where the time goes:
time: 81.9 us; the launch traced here: 81.7 us
  Pallas kernels  80 us (98%)
  local copies, waits for them, and re-layouts  1.67 us (2%)
    pallas_call x1, Pallas kernels, device_body(): pl.pallas_call(functools.partial(kernel, mesh.shape['row']), name='unet',...  80 us
    transpose x1, local copies, waits for them, and re-layouts, device_body(): return jnp.transpose(out, (0, 2, 1))  1.67 us

commit v1 on v0

--- a/solution.py
+++ b/solution.py
@@ -236,22 +236,42 @@
 
     LEVEL2 = [(a, b) for a in range(2) for b in range(2)]
 
-    def near(a, b):
-        return [(dy, dx) for dy, dx in ALL if dy != 2 * a and dx != 2 * b]
-
-    def weights_of(weight, taps):
-        return jnp.concatenate([weight[dy, dx] for dy, dx in taps], axis=0)
+    def plane_of(buf, a, b, line, lane, width):
+        return buf[a, b, pl.ds(line, SIDE), :, pl.ds(lane, width)].reshape(PIX, width)
+
+    def near(a, b, buf, weight, lane, width):
+        lhs = [plane_of(buf, k, l + 1, 1, lane, width) for k, l in LEVEL2]
+        rhs = [weight[k - a + 1, l - b + 1, lane:lane + width] for k, l in LEVEL2]
+        return dot(jnp.concatenate(lhs, axis=1), jnp.concatenate(rhs, axis=0))
+
+    def far(a, b, buf, weight, lane, width):
+        lhs = [plane_of(buf, 1 - a, b + dx, 2 * a, lane, width) for dx in range(3)]
+        lhs += [plane_of(buf, k, 3 * b, 1, lane, width) for k in range(2)]
+        rhs = [weight[2 * a, dx, lane:lane + width] for dx in range(3)]
+        rhs += [weight[k - a + 1, 2 * b, lane:lane + width] for k in range(2)]
+        return dot(jnp.concatenate(lhs, axis=1), jnp.concatenate(rhs, axis=0))
+
+    def over_level2(terms, put, *operands):
+        @pl.loop(0, 2)
+        def _(a):
+            for b in range(2):
+                put(a, b, terms(a, b, *operands))
+
+    def keep(a, b, value):
+        part[2 * a + b] = value
+
+    def add(a, b, value):
+        part[2 * a + b] += value
+
+    def done(bias, put):
+        return lambda a, b, value: put(a, b, biased_relu(part[2 * a + b] + value, bias))
 
     def conv_level2(index, src, weight, bias, put):
+        width = src.shape[-1]
         start(index, src)
-        for a, b in LEVEL2:
-            taps = near(a, b)
-            part[2 * a + b] = dot(gather(src, 2, a, (b,), taps), weights_of(weight, taps))
+        over_level2(near, keep, src, weight, 0, width)
         finish(index, src)
-        for a, b in LEVEL2:
-            taps = [tap for tap in ALL if tap not in near(a, b)]
-            acc = part[2 * a + b] + dot(gather(src, 2, a, (b,), taps), weights_of(weight, taps))
-            put(a, b, biased_relu(acc, bias))
+        over_level2(far, done(bias, put), src, weight, 0, width)
 
     at, to = grid_iota(HALF, HALF)
     split_cols = ones_at(at == lax.rem(to, SIDE) * 4 + to // SIDE)
@@ -327,9 +347,10 @@
             out = jnp.where(off.get(b, off_rows), 0.0, jnp.maximum(acc + bpad[0:1, :], 0.0))
             h1[a, b] = out.astype(BF16).reshape(ROWS, SIDE, C1P)
 
-    @pl.loop(0, 4)
-    def _(a):
-        put_planes(cat1, a, range(4), biased_relu(conv(h1, 4, a, range(4), ve1b), bpad.at[1:2]), LANE)
+    @pl.loop(0, 2)
+    def _(t):
+        for a in (2 * t, 2 * t + 1):
+            put_planes(cat1, a, range(4), biased_relu(conv(h1, 4, a, range(4), ve1b), bpad.at[1:2]), LANE)
 
     pool(cat1, p1, 2, LANE, C1P)
 
@@ -342,18 +363,14 @@
 
     start(POOL2, p2)
     start(SKIP2, cat2, C2)
+    copies[6].wait()
+    over_level2(near, keep, cat2, vd2a, C2, C2)
     copies[3].wait()
     finish(POOL2, p2)
     put_planes(ma, 0, (0,), biased_relu(conv(p2, 1, 0, (0,), vma), bma))
     start(MIDA, ma)
-    copies[6].wait()
     finish(SKIP2, cat2, C2)
-
-    def half_dec2a(a, lane):
-        flat = jnp.concatenate([vd2a[dy, dx, lane:lane + C2] for dy, dx in ALL], axis=0)
-        return dot(gather(cat2, 2, a, range(2), ALL, lane, C2), flat)
-
-    part[:2] = half_dec2a(0, C2).reshape(2, PIX, C2)
+    over_level2(far, add, cat2, vd2a, C2, C2)
     copies[4].wait()
     finish(MIDA, ma)
     mid[...] = biased_relu(conv(ma, 1, 0, (0,), vmb), bmb)
@@ -361,13 +378,9 @@
     for p, q in LEVEL2:
         put_planes(cat2, p, (q,), dot(mid[...], vu2[p, q]).astype(BF16))
     start(UP2, cat2)
-    part[2:] = half_dec2a(1, C2).reshape(2, PIX, C2)
+    over_level2(near, add, cat2, vd2a, 0, C2)
     finish(UP2, cat2)
-
-    @pl.loop(0, 2)
-    def _(a):
-        put_planes(e2a, a, range(2), biased_relu(part[pl.ds(2 * a, 2)].reshape(2 * PIX, C2) + half_dec2a(a, 0), bd2a))
-
+    over_level2(far, done(bd2a, lambda a, b, value: put_planes(e2a, a, (b,), value)), cat2, vd2a, 0, C2)
     copies[-1].wait()
 
     def put_d2(a, b, value):
@@ -376,22 +389,24 @@
     conv_level2(DEC2A, e2a, ve2b, bd2b, put_d2)
     copies[7].wait()
 
-    @pl.loop(0, 4)
+    @pl.loop(0, 2)
     def _(t):
-        p = lax.rem(t, 2)
-        lhs = d2[pl.ds((t - p) * PIX, 2 * PIX)]
-        for q in range(2):
-            put_planes(cat1, t, (q, q + 2), dot_rows(lhs, vu1[p, q]).astype(BF16))
+        lhs = d2[pl.ds(2 * t * PIX, 2 * PIX)]
+        for p, q in LEVEL2:
+            put_planes(cat1, 2 * t + p, (q, q + 2), dot_rows(lhs, vu1[p, q]).astype(BF16))
 
     for copy in copies[8:17]:
         copy.wait()
 
     def level1(index, src, layer):
         start(index, src)
-        pl.loop(1, 3)(lambda a: layer(a, (1, 2)))
+        for a in range(1, 3):
+            layer(a, (1, 2))
         finish(index, src)
-        pl.loop(1, 3)(lambda a: layer(a, (0, 3)))
-        pl.loop(0, 2)(lambda t: layer(3 * t, range(4)))
+        for a in range(1, 3):
+            layer(a, (0, 3))
+        for a in (0, 3):
+            layer(a, range(4))
 
     def dec1a(a, bs):
         put_planes(d1a, a, bs, biased_relu(dot_rows(gather(cat1, 4, a, bs, ALL), vd1a[...]), bpad.at[2:3]))
@@ -411,7 +426,7 @@
             picked = jnp.concatenate([h1[a, b + 1, lines, :, :C1].reshape(HALF, C1) for b in range(4)], axis=0)
             head = dot_rows(wh[...], dot(weave[...], picked).astype(BF16))
             for i in range(4):
-                y[4 * (4 * g + i) + a] = head[:, i * HALF:(i + 1) * HALF] + head_bias
+                y[:, 4 * (4 * g + i) + a, :] = head[:, i * HALF:(i + 1) * HALF] + head_bias
 
     level1(DEC1A, d1a, dec1b)
 
@@ -454,13 +469,13 @@
         out = pl.pallas_call(
             functools.partial(kernel, mesh.shape["row"]),
             name="unet",
-            out_shape=jax.ShapeDtypeStruct((HALF, 6, HALF), F32),
+            out_shape=jax.ShapeDtypeStruct((6, HALF, HALF), F32),
             in_specs=specs,
             out_specs=vmem,
             scratch_shapes=scratch,
             compiler_params=pltpu.CompilerParams(collective_id=0, has_side_effects=True, vmem_limit_bytes=67043328),
         )(*operands)
-        return jnp.transpose(out, (0, 2, 1))
+        return jnp.transpose(out, (1, 2, 0))
 
     def program(image, *params):
         mapped = jax.shard_map(device_body, mesh=mesh, in_specs=(tile_spec,) + tuple([P()] * len(params)), out_specs=tile_spec, check_vma=False)

time: 81.9 us -> 81.8 us (level)
    transpose x1 -> x0, local copies, waits for them, and re-layouts: 1.67 us -> none  [device_body(): return jnp.transpose(out, (0, 2, 1))]
    unnamed x0 -> x1, local copies, waits for them, and re-layouts: none -> 1.62 us
where the time goes in v1:
time: 81.8 us; the launch traced here: 81.7 us
  Pallas kernels  80 us (98%)
  local copies, waits for them, and re-layouts  1.62 us (2%)
    pallas_call x1, Pallas kernels, device_body(): pl.pallas_call(functools.partial(kernel, mesh.shape['row']), name='unet',...  80 us

profile of v1, /device:TPU:0, one launch (start us, length us, event | category | flops | bytes accessed | tf_op | source)
XLA Modules:
  0.0 81.7 jit_solution(6734850349768705213)
XLA Ops:
  0.0 80.0 %unet.1 = f32[6,64,64]{2,1,0:T(8,128)} custom-call(bf16[3,64,64]{2,1,0:T(8,128)(2,1)} %bitcast.8, bf16[3,3,3,192]{3,2,1,0:T(4,128)(2,1)} %we1a.1, bf16[3,3,192,192]{3,2,1,0:T(8,128)(2,1)} %we1b.1, bf16[3,3,192,384]{3,2,1,0:T(8,128)(2,1)} %we2a.1, bf16[3,3,384,384]{3,2,1,0:T(8,128)(2,1)} %we2b.1, bf16[3,3,384,768]{3,2,1,0:T(8,128)(2,1)} %wma.1, ...), custom_call_target="tpu_custom_call" | custom-call | tf_op jit(solution)/shard_map/unet/pallas_call | solution.py:469
  80.0 1.6 %copy.27 = f32[64,64,6]{1,0,2:T(8,128)} copy(f32[64,64,6]{1,0,2:T(8,128)} %bitcast.6) | data formatting | bytes 196608

commit v2 on v1

--- a/solution.py
+++ b/solution.py
@@ -23,8 +23,8 @@
 PATCH = 192
 TAPROWS = 40
 BY_ROWS = (((1,), (1,)), ((), ()))
-POOL1, ENC2A, POOL2, MIDA, UP2, DEC2A, CAT1, DEC1A, IMAGE, SKIP2 = range(10)
-EXCHANGE = ((2, C1P), (2, C2), (1, C2), (1, C3), (2, C2), (2, C2), (4, C2), (4, C1P), (1, LANE), (2, C2))
+POOL1, ENC2A, POOL2, MIDA, UP2, DEC2A, CAT1, DEC1A, IMAGE, SKIP2, SKIP1 = range(11)
+EXCHANGE = ((2, C1P), (2, C2), (1, C2), (1, C3), (2, C2), (2, C2), (4, C1P), (4, C1P), (1, LANE), (2, C2), (4, C1P))
 MESSAGES = 5
 LOADS = 19
 
@@ -54,9 +54,9 @@
 
 
 def kernel(row_count, x, we1a, we1b, we2a, we2b, wma, wmb, wu2, wd2a, wd2b, wu1, wd1a, wd1b, wh,
-           be1a, be1b, be2a, be2b, bma, bmb, bd2a, bd2b, bd1a, bd1b, bh, y, *scratch):
+           be1a, be1b, be2a, be2b, bma, bmb, bd2a, bd2b, bd1a, bd1b, y, *scratch):
     (vw8, re1b, ve1b, ve2a, ve2b, vma, vmb, vu2, vd2a, vu1, vd1a, vd1b,
-     h1, cat1, d1a, p1, e2a, cat2, d2, p2, ma, mid, x1, x8, wf, bpad, weave, part) = scratch[:-2 * len(EXCHANGE) - 3]
+     h1, cat1, d1a, p1, e2a, cat2, d2, p2, ma, mid, x1, x8, wf, bpad, weave, part, heads) = scratch[:-2 * len(EXCHANGE) - 3]
     send_cols = scratch[-2 * len(EXCHANGE) - 3:-len(EXCHANGE) - 3]
     recv_cols = scratch[-len(EXCHANGE) - 3:-3]
     w_sem, send_sem, recv_sem = scratch[-3:]
@@ -207,26 +207,28 @@
 
     ALL = [(dy, dx) for dy in range(3) for dx in range(3)]
 
-    def gather(buf, factor, a, bs, taps, lane=0, width=None):
-        lanes = pl.ds(lane, buf.shape[-1] if width is None else width)
+    def gather(buf, factor, planes):
         rows = []
-        for b in bs:
+        for a, b in planes:
             parts = []
-            for dy, dx in taps:
+            for dy, dx in ALL:
                 shifted = a + (dy - 1 + factor)
-                piece = buf[lax.rem(shifted, factor), b + dx, pl.ds(shifted // factor, SIDE), :, lanes]
+                piece = buf[lax.rem(shifted, factor), b + dx, pl.ds(shifted // factor, SIDE)]
                 parts.append(piece.reshape(PIX, piece.shape[-1]))
             rows.append(jnp.concatenate(parts, axis=1))
         return jnp.concatenate(rows, axis=0)
 
-    def conv(buf, factor, a, bs, weight):
-        return dot(gather(buf, factor, a, bs, ALL), weight[...].reshape(9 * buf.shape[-1], weight.shape[-1]))
-
-    def put_planes(buf, a, bs, value, lane=0):
+    def conv(buf, factor, planes, weight):
+        return dot(gather(buf, factor, planes), weight[...].reshape(9 * buf.shape[-1], weight.shape[-1]))
+
+    def put_planes(buf, planes, value, lane=0):
         width = value.shape[-1]
-        for k, b in enumerate(bs):
+        for k, (a, b) in enumerate(planes):
             plane = value[k * PIX:(k + 1) * PIX].reshape(SIDE, SIDE, width)
             buf[a, b + 1, 1:ROWS - 1, :, lane:lane + width] = plane
+
+    def row_of(a):
+        return [(a, b) for b in range(4)]
 
     def pool(src, dst, factor, lane, width):
         for a in range(factor):
@@ -266,10 +268,14 @@
     def done(bias, put):
         return lambda a, b, value: put(a, b, biased_relu(part[2 * a + b] + value, bias))
 
-    def conv_level2(index, src, weight, bias, put):
+    def conv_level2(index, src, weight, bias, put, first=None, then=None):
         width = src.shape[-1]
         start(index, src)
+        if first is not None:
+            first()
         over_level2(near, keep, src, weight, 0, width)
+        if then is not None:
+            then()
         finish(index, src)
         over_level2(far, done(bias, put), src, weight, 0, width)
 
@@ -306,11 +312,6 @@
     bpad[0:1, :] = jnp.concatenate([be1a[...].reshape(1, C1), pad], axis=1)
     bpad[1:2, :] = jnp.concatenate([pad, be1b[...].reshape(1, C1)], axis=1)
     bpad[2:3, :] = jnp.concatenate([bd1a[...].reshape(1, C1), pad], axis=1)
-    n, m = grid_iota(PIX, PIX)
-    weave[...] = ones_at(m == lax.rem(n, 4) * HALF + (n // HALF) * SIDE + lax.rem(n, HALF) // 4)
-    ve2a[:, :, :HALF, :] = jnp.zeros((3, 3, HALF, C2), BF16)
-    vd1b[:, :, C1:, :] = jnp.zeros((3, 3, HALF, C1), BF16)
-    vd1a[C1:, :] = jnp.zeros((HALF, vd1a.shape[1]), BF16)
     copies[0].wait()
 
     @pl.loop(0, 3)
@@ -350,14 +351,25 @@
     @pl.loop(0, 2)
     def _(t):
         for a in (2 * t, 2 * t + 1):
-            put_planes(cat1, a, range(4), biased_relu(conv(h1, 4, a, range(4), ve1b), bpad.at[1:2]), LANE)
+            put_planes(cat1, row_of(a), biased_relu(conv(h1, 4, row_of(a), ve1b), bpad.at[1:2]), LANE)
 
     pool(cat1, p1, 2, LANE, C1P)
 
+    ve2a[:, :, :HALF, :] = jnp.zeros((3, 3, HALF, C2), BF16)
+
+    def fill_constants():
+        start(SKIP1, cat1, LANE)
+        n, m = grid_iota(2 * PIX, 2 * PIX)
+        weave[...] = ones_at(m == lax.rem(n, 4) * LANE + (n // HALF) * SIDE + lax.rem(n, HALF) // 4)
+        vd1b[:, :, C1:, :] = jnp.zeros((3, 3, HALF, C1), BF16)
+        vd1a[C1:, :] = jnp.zeros((HALF, vd1a.shape[1]), BF16)
+        heads[...] = jnp.zeros(heads.shape, F32)
+
     copies[1].wait()
-    conv_level2(POOL1, p1, ve2a, be2a, lambda a, b, value: put_planes(e2a, a, (b,), value))
+    conv_level2(POOL1, p1, ve2a, be2a, lambda a, b, value: put_planes(e2a, [(a, b)], value), first=fill_constants)
     copies[2].wait()
-    conv_level2(ENC2A, e2a, ve2b, be2b, lambda a, b, value: put_planes(cat2, a, (b,), value, C2))
+    conv_level2(ENC2A, e2a, ve2b, be2b, lambda a, b, value: put_planes(cat2, [(a, b)], value, C2),
+                then=lambda: finish(SKIP1, cat1, LANE))
     copies[-1].start()
     pool(cat2, p2, 1, C2, C2)
 
@@ -367,20 +379,22 @@
     over_level2(near, keep, cat2, vd2a, C2, C2)
     copies[3].wait()
     finish(POOL2, p2)
-    put_planes(ma, 0, (0,), biased_relu(conv(p2, 1, 0, (0,), vma), bma))
+    put_planes(ma, [(0, 0)], biased_relu(conv(p2, 1, [(0, 0)], vma), bma))
     start(MIDA, ma)
     finish(SKIP2, cat2, C2)
     over_level2(far, add, cat2, vd2a, C2, C2)
     copies[4].wait()
     finish(MIDA, ma)
-    mid[...] = biased_relu(conv(ma, 1, 0, (0,), vmb), bmb)
+    mid[...] = biased_relu(conv(ma, 1, [(0, 0)], vmb), bmb)
     copies[5].wait()
-    for p, q in LEVEL2:
-        put_planes(cat2, p, (q,), dot(mid[...], vu2[p, q]).astype(BF16))
+    for p in range(2):
+        out = dot(mid[...], jnp.concatenate([vu2[p, 0], vu2[p, 1]], axis=1)).astype(BF16)
+        for q in range(2):
+            put_planes(cat2, [(p, q)], out[:, q * C2:(q + 1) * C2])
     start(UP2, cat2)
     over_level2(near, add, cat2, vd2a, 0, C2)
     finish(UP2, cat2)
-    over_level2(far, done(bd2a, lambda a, b, value: put_planes(e2a, a, (b,), value)), cat2, vd2a, 0, C2)
+    over_level2(far, done(bd2a, lambda a, b, value: put_planes(e2a, [(a, b)], value)), cat2, vd2a, 0, C2)
     copies[-1].wait()
 
     def put_d2(a, b, value):
@@ -393,42 +407,49 @@
     def _(t):
         lhs = d2[pl.ds(2 * t * PIX, 2 * PIX)]
         for p, q in LEVEL2:
-            put_planes(cat1, 2 * t + p, (q, q + 2), dot_rows(lhs, vu1[p, q]).astype(BF16))
+            put_planes(cat1, [(2 * t + p, q), (2 * t + p, q + 2)], dot_rows(lhs, vu1[p, q]).astype(BF16))
 
     for copy in copies[8:17]:
         copy.wait()
 
+    border = 3 * col
+
     def level1(index, src, layer):
         start(index, src)
-        for a in range(1, 3):
-            layer(a, (1, 2))
+        for a in (1, 2):
+            layer([(a, 1), (a, 2), (a, border)])
         finish(index, src)
-        for a in range(1, 3):
-            layer(a, (0, 3))
+        layer([(1, 3 - border), (2, 3 - border)])
         for a in (0, 3):
-            layer(a, range(4))
-
-    def dec1a(a, bs):
-        put_planes(d1a, a, bs, biased_relu(dot_rows(gather(cat1, 4, a, bs, ALL), vd1a[...]), bpad.at[2:3]))
+            layer(row_of(a))
+
+    def dec1a(planes):
+        put_planes(d1a, planes, biased_relu(dot_rows(gather(cat1, 4, planes), vd1a[...]), bpad.at[2:3]))
 
     level1(CAT1, cat1, dec1a)
     copies[17].wait()
-    head_bias = jnp.zeros((6, HALF), F32)
-    for c in range(6):
-        head_bias = jnp.where(iota(head_bias.shape, 0) == c, bh[c], head_bias)
-
-    def dec1b(a, bs):
-        put_planes(h1, a, bs, biased_relu(conv(d1a, 4, a, bs, vd1b), bd1b))
-        if 0 not in bs:
-            return
-        for g in range(4):
-            lines = pl.ds(4 * g + 1, 4)
-            picked = jnp.concatenate([h1[a, b + 1, lines, :, :C1].reshape(HALF, C1) for b in range(4)], axis=0)
-            head = dot_rows(wh[...], dot(weave[...], picked).astype(BF16))
-            for i in range(4):
-                y[:, 4 * (4 * g + i) + a, :] = head[:, i * HALF:(i + 1) * HALF] + head_bias
+
+    def head(a):
+        lines = [h1[a, b + 1, pl.ds(8 * h + 1, 8), :, :C1].reshape(LANE, C1) for h in range(2) for b in range(4)]
+        heads[a, :6] = dot_rows(wh[...], jnp.concatenate(lines, axis=0))
+
+    def dec1b(planes):
+        put_planes(h1, planes, biased_relu(conv(d1a, 4, planes, vd1b), bd1b))
 
     level1(DEC1A, d1a, dec1b)
+    for a in range(4):
+        head(a)
+    wide = 2 * PIX
+    flat = jnp.concatenate([heads[a, :, h * wide:(h + 1) * wide] for a in range(4) for h in range(2)], axis=0)
+    high = flat.astype(BF16)
+    rest = flat - high.astype(F32)
+    middle = rest.astype(BF16)
+    low = (rest - middle.astype(F32)).astype(BF16)
+    woven = dot_rows(high, weave[...]) + dot_rows(middle, weave[...]) + dot_rows(low, weave[...])
+    for a in range(4):
+        for h in range(2):
+            for i in range(8):
+                y[:, 4 * (8 * h + i) + a, :] = woven[(2 * a + h) * 8:(2 * a + h) * 8 + 6, i * HALF:(i + 1) * HALF]
 
 
 def solution(mesh):
@@ -443,9 +464,9 @@
         operands = [
             jnp.transpose(image_tile, (2, 0, 1)), w_enc1a, w_enc1b, w_enc2a, w_enc2b, w_mid_a, w_mid_b,
             w_up2, w_dec2a, w_dec2b, jnp.swapaxes(w_up1, 2, 3), jnp.swapaxes(w_dec1a, 2, 3), w_dec1b, w_head.T,
-            b_enc1a, b_enc1b, b_enc2a, b_enc2b, b_mid_a, b_mid_b, b_dec2a, b_dec2b, b_dec1a, b_dec1b, b_head,
+            b_enc1a, b_enc1b, b_enc2a, b_enc2b, b_mid_a, b_mid_b, b_dec2a, b_dec2b, b_dec1a, b_dec1b,
         ]
-        specs = [vmem] * 2 + [anywhere] * 11 + [vmem] * 11 + [pl.BlockSpec(memory_space=pltpu.SMEM)]
+        specs = [vmem] * 2 + [anywhere] * 11 + [vmem] * 11
 
         def kept(*shape, dtype=BF16):
             return pltpu.VMEM(shape, dtype)
@@ -459,8 +480,8 @@
             kept(2, 2, C1, C2), kept(C1P, 9 * C2), kept(3, 3, C1P, C1),
             level(4, C1P), level(4, C2), level(4, C1P), level(2, C1P), level(2, C2), level(2, C3),
             kept(4 * PIX, C2), level(1, C2), level(1, C3), kept(PIX, C3), level(1, LANE), kept(EXT, PATCH),
-            kept(TAPROWS, C1P, dtype=F32), kept(3, C1P, dtype=F32), kept(PIX, PIX),
-            kept(4, PIX, C2, dtype=F32),
+            kept(TAPROWS, C1P, dtype=F32), kept(3, C1P, dtype=F32), kept(2 * PIX, 2 * PIX),
+            kept(4, PIX, C2, dtype=F32), kept(4, 8, 4 * PIX, dtype=F32),
         ]
         scratch += [kept(factor, SIDE, width) for factor, width in EXCHANGE]
         scratch += [kept(factor + 2, SIDE, width) for factor, width in EXCHANGE]
@@ -475,7 +496,7 @@
             scratch_shapes=scratch,
             compiler_params=pltpu.CompilerParams(collective_id=0, has_side_effects=True, vmem_limit_bytes=67043328),
         )(*operands)
-        return jnp.transpose(out, (1, 2, 0))
+        return jnp.transpose(out, (1, 2, 0)) + b_head
 
     def program(image, *params):
         mapped = jax.shard_map(device_body, mesh=mesh, in_specs=(tile_spec,) + tuple([P()] * len(params)), out_specs=tile_spec, check_vma=False)

time: 81.8 us -> 75.3 us (0.921)
  Pallas kernels: 80 us -> 73.4 us
  other arithmetic: 0 us -> 1.69 us
  local copies, waits for them, and re-layouts: 1.62 us -> 0 us
    pallas_call x1, Pallas kernels: 80 us -> 73.4 us  [device_body(): pl.pallas_call(functools.partial(kernel, mesh.shape['row']), name='unet',...]
    add x0 -> x1, other arithmetic: none -> 1.69 us  [device_body(): return jnp.transpose(out, (1, 2, 0)) + b_head]
    unnamed x1 -> x0, local copies, waits for them, and re-layouts: 1.62 us -> none
where the time goes in v2:
time: 75.3 us; the launch traced here: 75.1 us
  Pallas kernels  73.4 us (97%)
  other arithmetic  1.69 us (2%)
    pallas_call x1, Pallas kernels, device_body(): pl.pallas_call(functools.partial(kernel, mesh.shape['row']), name='unet',...  73.4 us
    add x1, other arithmetic, device_body(): return jnp.transpose(out, (1, 2, 0)) + b_head  1.69 us

profile of v2, /device:TPU:0, one launch (start us, length us, event | category | flops | bytes accessed | tf_op | source)
XLA Modules:
  0.0 75.1 jit_solution(7583357512611438212)
XLA Ops:
  0.0 73.4 %unet.1 = f32[6,64,64]{2,1,0:T(8,128)} custom-call(bf16[3,64,64]{2,1,0:T(8,128)(2,1)} %bitcast.8, bf16[3,3,3,192]{3,2,1,0:T(4,128)(2,1)} %we1a.1, bf16[3,3,192,192]{3,2,1,0:T(8,128)(2,1)} %we1b.1, bf16[3,3,192,384]{3,2,1,0:T(8,128)(2,1)} %we2a.1, bf16[3,3,384,384]{3,2,1,0:T(8,128)(2,1)} %we2b.1, bf16[3,3,384,768]{3,2,1,0:T(8,128)(2,1)} %wma.1, ...), custom_call_target="tpu_custom_call" | custom-call | tf_op jit(solution)/shard_map/unet/pallas_call | solution.py:490
  73.5 1.7 %add_bitcast_fusion = f32[64,64,6]{1,0,2:T(8,128)} fusion(f32[6,64,64]{2,1,0:T(8,128)} %unet.1, f32[6]{0:T(128)} %param.49), kind=kLoop, calls=%fused_computation | loop fusion | flops 24576 | bytes 196632 | tf_op jit(solution)/shard_map/add | solution.py:499

commit v3 on v2

--- a/solution.py
+++ b/solution.py
@@ -67,6 +67,23 @@
     side, side_up, side_down = (data, 1 - col, row), (data, 1 - col, row - 1), (data, 1 - col, row + 1)
     edge = (1 - col) * (SIDE - 1)
 
+    barrier = pltpu.get_barrier_semaphore()
+
+    def arrive(device):
+        pl.semaphore_signal(barrier, inc=1, device_id=device, device_id_type=MESH)
+
+    arrive(side)
+
+    @pl.when(has_up)
+    def _():
+        arrive(up)
+        arrive(side_up)
+
+    @pl.when(has_down)
+    def _():
+        arrive(down)
+        arrive(side_down)
+
     loads = [(we1b, re1b), (we2a, ve2a.at[:, :, HALF:, :]), (we2b, ve2b), (wma, vma), (wmb, vmb),
              (wu2, vu2), (wd2a, vd2a), (wu1, vu1)]
     loads += [(wd1a.at[t // 3, t % 3], vd1a.at[:C1, pl.ds(t * C2, C2)]) for t in range(9)]
@@ -74,30 +91,6 @@
     copies = [pltpu.make_async_copy(src, dst, w_sem.at[k]) for k, (src, dst) in enumerate(loads)]
     for copy in copies[:3]:
         copy.start()
-    for buf, factor in ((h1, 4), (cat1, 4), (d1a, 4), (p1, 2), (e2a, 2), (cat2, 2), (p2, 1), (ma, 1), (x1, 1)):
-        blank = jnp.zeros(buf.shape[1:2] + buf.shape[3:], BF16)
-        buf[0, :, ROWS - 1] = blank
-        buf[factor - 1, :, 0] = blank
-    for buf, (factor, _) in zip(recv_cols, EXCHANGE):
-        buf[factor:] = jnp.zeros((2,) + buf.shape[1:], BF16)
-
-    barrier = pltpu.get_barrier_semaphore()
-
-    def arrive(device):
-        pl.semaphore_signal(barrier, inc=1, device_id=device, device_id_type=MESH)
-
-    arrive(side)
-
-    @pl.when(has_up)
-    def _():
-        arrive(up)
-        arrive(side_up)
-
-    @pl.when(has_down)
-    def _():
-        arrive(down)
-        arrive(side_down)
-
     for copy in copies[3:-1]:
         copy.start()
 
@@ -241,23 +234,27 @@
     def plane_of(buf, a, b, line, lane, width):
         return buf[a, b, pl.ds(line, SIDE), :, pl.ds(lane, width)].reshape(PIX, width)
 
-    def near(a, b, buf, weight, lane, width):
+    def near(a, buf, weight, lane, width):
         lhs = [plane_of(buf, k, l + 1, 1, lane, width) for k, l in LEVEL2]
-        rhs = [weight[k - a + 1, l - b + 1, lane:lane + width] for k, l in LEVEL2]
-        return dot(jnp.concatenate(lhs, axis=1), jnp.concatenate(rhs, axis=0))
-
-    def far(a, b, buf, weight, lane, width):
-        lhs = [plane_of(buf, 1 - a, b + dx, 2 * a, lane, width) for dx in range(3)]
-        lhs += [plane_of(buf, k, 3 * b, 1, lane, width) for k in range(2)]
-        rhs = [weight[2 * a, dx, lane:lane + width] for dx in range(3)]
-        rhs += [weight[k - a + 1, 2 * b, lane:lane + width] for k in range(2)]
-        return dot(jnp.concatenate(lhs, axis=1), jnp.concatenate(rhs, axis=0))
+        both = [jnp.concatenate([weight[k - a + 1, l - b + 1, lane:lane + width] for k, l in LEVEL2], axis=0) for b in range(2)]
+        out = dot(jnp.concatenate(lhs, axis=1), jnp.concatenate(both, axis=1))
+        return out[:, :C2], out[:, C2:]
+
+    def far(a, buf, weight, lane, width):
+        outs = []
+        for b in range(2):
+            lhs = [plane_of(buf, 1 - a, b + dx, 2 * a, lane, width) for dx in range(3)]
+            lhs += [plane_of(buf, k, 3 * b, 1, lane, width) for k in range(2)]
+            rhs = [weight[2 * a, dx, lane:lane + width] for dx in range(3)]
+            rhs += [weight[k - a + 1, 2 * b, lane:lane + width] for k in range(2)]
+            outs.append(dot(jnp.concatenate(lhs, axis=1), jnp.concatenate(rhs, axis=0)))
+        return outs
 
     def over_level2(terms, put, *operands):
         @pl.loop(0, 2)
         def _(a):
-            for b in range(2):
-                put(a, b, terms(a, b, *operands))
+            for b, value in enumerate(terms(a, *operands)):
+                put(a, b, value)
 
     def keep(a, b, value):
         part[2 * a + b] = value
@@ -294,6 +291,23 @@
     x1[0, 1, 1:ROWS - 1] = sum(image[1:], image[0]).astype(BF16).reshape(SIDE, SIDE, LANE)
     start(IMAGE, x1)
 
+    mapped = ((cat1, 4), (d1a, 4), (p1, 2), (e2a, 2), (cat2, 2), (p2, 1), (ma, 1), (x1, 1))
+
+    @pl.when(row == 0)
+    def _():
+        for buf, factor in mapped:
+            buf[factor - 1, :, 0] = jnp.zeros(buf.shape[1:2] + buf.shape[3:], BF16)
+        for buf, (factor, _) in zip(recv_cols, EXCHANGE):
+            buf[factor] = jnp.zeros(buf.shape[1:], BF16)
+
+    @pl.when(row == last)
+    def _():
+        for buf, factor in mapped:
+            buf[0, :, ROWS - 1] = jnp.zeros(buf.shape[1:2] + buf.shape[3:], BF16)
+        for buf, (factor, _) in zip(recv_cols, EXCHANGE):
+            buf[factor + 1] = jnp.zeros(buf.shape[1:], BF16)
+
+
     wf[...] = jnp.zeros(wf.shape, F32)
     for t in range(9):
         wf[pl.ds(4 * t, 3), :C1] = we1a[t // 3, t % 3].astype(F32)
@@ -309,9 +323,11 @@
             vw8[a * 6 + b] = dot(place, wf[...].astype(BF16)).astype(BF16)
 
     pad = jnp.zeros((1, HALF), F32)
-    bpad[0:1, :] = jnp.concatenate([be1a[...].reshape(1, C1), pad], axis=1)
-    bpad[1:2, :] = jnp.concatenate([pad, be1b[...].reshape(1, C1)], axis=1)
-    bpad[2:3, :] = jnp.concatenate([bd1a[...].reshape(1, C1), pad], axis=1)
+    bpad[0:1, :C1P] = jnp.concatenate([be1a[...].reshape(1, C1), pad], axis=1)
+    bpad[1:2, :C1P] = jnp.concatenate([pad, be1b[...].reshape(1, C1)], axis=1)
+    bpad[2:3, :C1P] = jnp.concatenate([bd1a[...].reshape(1, C1), pad], axis=1)
+    bpad[3:4, :] = bma[...].reshape(1, C3)
+    bpad[4:5, :] = bmb[...].reshape(1, C3)
     copies[0].wait()
 
     @pl.loop(0, 3)
@@ -337,21 +353,29 @@
     x8[...] = sum(patches[1:], patches[0]).astype(BF16)
 
     pos = iota((EXT, C1P), 0)
-    pos_row, pos_col = pos // SIDE, lax.rem(pos, SIDE)
-    off_rows = ((pos_row == 0) & (row == 0)) | ((pos_row == ROWS - 1) & (row == last))
-    off = {0: off_rows | ((pos_col == 0) & (col == 0)), 5: off_rows | ((pos_col == SIDE - 1) & (col == 1))}
+    pos_col = lax.rem(pos, SIDE)
+    off = {0: (pos_col == 0) & (col == 0), 5: (pos_col == SIDE - 1) & (col == 1)}
 
     @pl.loop(0, 4)
     def _(a):
         for b in range(6):
-            acc = dot(x8[...], vw8[a * 6 + b])
-            out = jnp.where(off.get(b, off_rows), 0.0, jnp.maximum(acc + bpad[0:1, :], 0.0))
+            out = jnp.maximum(dot(x8[...], vw8[a * 6 + b]) + bpad[0:1, :C1P], 0.0)
+            if b in off:
+                out = jnp.where(off[b], 0.0, out)
             h1[a, b] = out.astype(BF16).reshape(ROWS, SIDE, C1P)
+
+    @pl.when(row == 0)
+    def _():
+        h1[3, :, 0] = jnp.zeros((6, SIDE, C1P), BF16)
+
+    @pl.when(row == last)
+    def _():
+        h1[0, :, ROWS - 1] = jnp.zeros((6, SIDE, C1P), BF16)
 
     @pl.loop(0, 2)
     def _(t):
         for a in (2 * t, 2 * t + 1):
-            put_planes(cat1, row_of(a), biased_relu(conv(h1, 4, row_of(a), ve1b), bpad.at[1:2]), LANE)
+            put_planes(cat1, row_of(a), biased_relu(conv(h1, 4, row_of(a), ve1b), bpad.at[1:2, :C1P]), LANE)
 
     pool(cat1, p1, 2, LANE, C1P)
 
@@ -379,13 +403,27 @@
     over_level2(near, keep, cat2, vd2a, C2, C2)
     copies[3].wait()
     finish(POOL2, p2)
-    put_planes(ma, [(0, 0)], biased_relu(conv(p2, 1, [(0, 0)], vma), bma))
+
+    def conv_level3(src, weight, bias, put):
+        @pl.loop(0, 3)
+        def _(n):
+            lanes = pl.ds(pl.multiple_of(n * PIX, PIX), PIX)
+            flat = weight[:, :, :, lanes].reshape(9 * src.shape[-1], PIX)
+            put(lanes, biased_relu(dot(gather(src, 1, [(0, 0)]), flat), bpad.at[bias:bias + 1, lanes]))
+
+    def put_ma(lanes, value):
+        ma[0, 1, 1:ROWS - 1, :, lanes] = value.reshape(SIDE, SIDE, PIX)
+
+    def put_mid(lanes, value):
+        mid[:, lanes] = value
+
+    conv_level3(p2, vma, 3, put_ma)
     start(MIDA, ma)
     finish(SKIP2, cat2, C2)
     over_level2(far, add, cat2, vd2a, C2, C2)
     copies[4].wait()
     finish(MIDA, ma)
-    mid[...] = biased_relu(conv(ma, 1, [(0, 0)], vmb), bmb)
+    conv_level3(ma, vmb, 4, put_mid)
     copies[5].wait()
     for p in range(2):
         out = dot(mid[...], jnp.concatenate([vu2[p, 0], vu2[p, 1]], axis=1)).astype(BF16)
@@ -424,7 +462,7 @@
             layer(row_of(a))
 
     def dec1a(planes):
-        put_planes(d1a, planes, biased_relu(dot_rows(gather(cat1, 4, planes), vd1a[...]), bpad.at[2:3]))
+        put_planes(d1a, planes, biased_relu(dot_rows(gather(cat1, 4, planes), vd1a[...]), bpad.at[2:3, :C1P]))
 
     level1(CAT1, cat1, dec1a)
     copies[17].wait()
@@ -480,7 +518,7 @@
             kept(2, 2, C1, C2), kept(C1P, 9 * C2), kept(3, 3, C1P, C1),
             level(4, C1P), level(4, C2), level(4, C1P), level(2, C1P), level(2, C2), level(2, C3),
             kept(4 * PIX, C2), level(1, C2), level(1, C3), kept(PIX, C3), level(1, LANE), kept(EXT, PATCH),
-            kept(TAPROWS, C1P, dtype=F32), kept(3, C1P, dtype=F32), kept(2 * PIX, 2 * PIX),
+            kept(TAPROWS, C1P, dtype=F32), kept(5, C3, dtype=F32), kept(2 * PIX, 2 * PIX),
             kept(4, PIX, C2, dtype=F32), kept(4, 8, 4 * PIX, dtype=F32),
         ]
         scratch += [kept(factor, SIDE, width) for factor, width in EXCHANGE]

time: 75.3 us -> 74.3 us (0.987)
  Pallas kernels: 73.4 us -> 72.4 us
    pallas_call x1, Pallas kernels: 73.4 us -> 72.4 us  [device_body(): pl.pallas_call(functools.partial(kernel, mesh.shape['row']), name='unet',...]
where the time goes in v3:
time: 74.3 us; the launch traced here: 74.1 us
  Pallas kernels  72.4 us (97%)
  other arithmetic  1.69 us (2%)
    pallas_call x1, Pallas kernels, device_body(): pl.pallas_call(functools.partial(kernel, mesh.shape['row']), name='unet',...  72.4 us
    add x1, other arithmetic, device_body(): return jnp.transpose(out, (1, 2, 0)) + b_head  1.69 us

profile of v3, /device:TPU:0, one launch (start us, length us, event | category | flops | bytes accessed | tf_op | source)
XLA Modules:
  0.0 74.1 jit_solution(3252965386612342107)
XLA Ops:
  0.0 72.4 %unet.1 = f32[6,64,64]{2,1,0:T(8,128)} custom-call(bf16[3,64,64]{2,1,0:T(8,128)(2,1)} %bitcast.8, bf16[3,3,3,192]{3,2,1,0:T(4,128)(2,1)} %we1a.1, bf16[3,3,192,192]{3,2,1,0:T(8,128)(2,1)} %we1b.1, bf16[3,3,192,384]{3,2,1,0:T(8,128)(2,1)} %we2a.1, bf16[3,3,384,384]{3,2,1,0:T(8,128)(2,1)} %we2b.1, bf16[3,3,384,768]{3,2,1,0:T(8,128)(2,1)} %wma.1, ...), custom_call_target="tpu_custom_call" | custom-call | tf_op jit(solution)/shard_map/unet/pallas_call | solution.py:528
  72.4 1.7 %add_bitcast_fusion = f32[64,64,6]{1,0,2:T(8,128)} fusion(f32[6,64,64]{2,1,0:T(8,128)} %unet.1, f32[6]{0:T(128)} %param.49), kind=kLoop, calls=%fused_computation | loop fusion | flops 24576 | bytes 196632 | tf_op jit(solution)/shard_map/add | solution.py:537

commit v4 on v3

--- a/solution.py
+++ b/solution.py
@@ -27,6 +27,7 @@
 EXCHANGE = ((2, C1P), (2, C2), (1, C2), (1, C3), (2, C2), (2, C2), (4, C1P), (4, C1P), (1, LANE), (2, C2), (4, C1P))
 MESSAGES = 5
 LOADS = 19
+SMALL = 13
 
 
 def iota(shape, dim):
@@ -53,8 +54,14 @@
     return jnp.maximum(acc + bias[...].reshape(1, bias.shape[-1]), 0.0).astype(BF16)
 
 
-def kernel(row_count, x, we1a, we1b, we2a, we2b, wma, wmb, wu2, wd2a, wd2b, wu1, wd1a, wd1b, wh,
-           be1a, be1b, be2a, be2b, bma, bmb, bd2a, bd2b, bd1a, bd1b, y, *scratch):
+def kernel(row_count, we1b, we2a, we2b, wma, wmb, wu2, wd2a, wd2b, wu1, wd1a, wd1b, *scratch):
+    small, y, scratch = scratch[:SMALL], scratch[SMALL], scratch[SMALL + 1:]
+    near_small, scratch = scratch[:SMALL], scratch[SMALL:]
+    x, we1a, wh, be1a, be1b, be2a, be2b, bma, bmb, bd2a, bd2b, bd1a, bd1b = near_small
+    small_sem, scratch = scratch[-1], scratch[:-1]
+    small_copies = [pltpu.make_async_copy(src, dst, small_sem.at[k]) for k, (src, dst) in enumerate(zip(small, near_small))]
+    for copy in small_copies:
+        copy.start()
     (vw8, re1b, ve1b, ve2a, ve2b, vma, vmb, vu2, vd2a, vu1, vd1a, vd1b,
      h1, cat1, d1a, p1, e2a, cat2, d2, p2, ma, mid, x1, x8, wf, bpad, weave, part, heads) = scratch[:-2 * len(EXCHANGE) - 3]
     send_cols = scratch[-2 * len(EXCHANGE) - 3:-len(EXCHANGE) - 3]
@@ -240,24 +247,28 @@
         out = dot(jnp.concatenate(lhs, axis=1), jnp.concatenate(both, axis=1))
         return out[:, :C2], out[:, C2:]
 
-    def far(a, buf, weight, lane, width):
-        outs = []
-        for b in range(2):
-            lhs = [plane_of(buf, 1 - a, b + dx, 2 * a, lane, width) for dx in range(3)]
-            lhs += [plane_of(buf, k, 3 * b, 1, lane, width) for k in range(2)]
-            rhs = [weight[2 * a, dx, lane:lane + width] for dx in range(3)]
-            rhs += [weight[k - a + 1, 2 * b, lane:lane + width] for k in range(2)]
-            outs.append(dot(jnp.concatenate(lhs, axis=1), jnp.concatenate(rhs, axis=0)))
-        return outs
-
-    def over_level2(terms, put, *operands):
+    def sides(a, b, buf, weight, lane, width):
+        lhs = [plane_of(buf, k, 3 * b, 1, lane, width) for k in range(2)]
+        rhs = [weight[k - a + 1, 2 * b, lane:lane + width] for k in range(2)]
+        return dot(jnp.concatenate(lhs, axis=1), jnp.concatenate(rhs, axis=0))
+
+    def far_rows(a, b, buf, weight, lane, width):
+        lhs = [plane_of(buf, 1 - a, b + dx, 2 * a, lane, width) for dx in range(3)]
+        rhs = [weight[2 * a, dx, lane:lane + width] for dx in range(3)]
+        return dot(jnp.concatenate(lhs, axis=1), jnp.concatenate(rhs, axis=0))
+
+    def near_sums(again, *operands):
         @pl.loop(0, 2)
         def _(a):
-            for b, value in enumerate(terms(a, *operands)):
-                put(a, b, value)
-
-    def keep(a, b, value):
-        part[2 * a + b] = value
+            for b, value in enumerate(near(a, *operands)):
+                part[2 * a + b] = part[2 * a + b] + value if again else value
+            part[2 * a + col] += sides(a, col, *operands)
+
+    def far_sums(put, *operands):
+        for a in range(2):
+            part[2 * a + 1 - col] += sides(a, 1 - col, *operands)
+            for b in range(2):
+                put(a, b, far_rows(a, b, *operands))
 
     def add(a, b, value):
         part[2 * a + b] += value
@@ -270,17 +281,18 @@
         start(index, src)
         if first is not None:
             first()
-        over_level2(near, keep, src, weight, 0, width)
+        near_sums(False, src, weight, 0, width)
         if then is not None:
             then()
         finish(index, src)
-        over_level2(far, done(bias, put), src, weight, 0, width)
+        far_sums(done(bias, put), src, weight, 0, width)
 
     at, to = grid_iota(HALF, HALF)
     split_cols = ones_at(at == lax.rem(to, SIDE) * 4 + to // SIDE)
     at, to = grid_iota(PIX, HALF)
     own_col = lax.rem(at, SIDE) == lax.rem(to, SIDE)
     fold_at, fold_to = grid_iota(HALF, LANE)
+    small_copies[0].wait()
     image = []
     for ch in range(3):
         cols = dot(x[ch], split_cols).astype(BF16)
@@ -307,6 +319,9 @@
         for buf, (factor, _) in zip(recv_cols, EXCHANGE):
             buf[factor + 1] = jnp.zeros(buf.shape[1:], BF16)
 
+
+    for copy in small_copies[1:]:
+        copy.wait()
 
     wf[...] = jnp.zeros(wf.shape, F32)
     for t in range(9):
@@ -356,9 +371,9 @@
     pos_col = lax.rem(pos, SIDE)
     off = {0: (pos_col == 0) & (col == 0), 5: (pos_col == SIDE - 1) & (col == 1)}
 
-    @pl.loop(0, 4)
-    def _(a):
-        for b in range(6):
+    @pl.loop(0, 2)
+    def _(t):
+        for a, b in [(2 * t + k, b) for k in range(2) for b in range(6)]:
             out = jnp.maximum(dot(x8[...], vw8[a * 6 + b]) + bpad[0:1, :C1P], 0.0)
             if b in off:
                 out = jnp.where(off[b], 0.0, out)
@@ -400,7 +415,7 @@
     start(POOL2, p2)
     start(SKIP2, cat2, C2)
     copies[6].wait()
-    over_level2(near, keep, cat2, vd2a, C2, C2)
+    near_sums(False, cat2, vd2a, C2, C2)
     copies[3].wait()
     finish(POOL2, p2)
 
@@ -420,7 +435,7 @@
     conv_level3(p2, vma, 3, put_ma)
     start(MIDA, ma)
     finish(SKIP2, cat2, C2)
-    over_level2(far, add, cat2, vd2a, C2, C2)
+    far_sums(add, cat2, vd2a, C2, C2)
     copies[4].wait()
     finish(MIDA, ma)
     conv_level3(ma, vmb, 4, put_mid)
@@ -430,9 +445,9 @@
         for q in range(2):
             put_planes(cat2, [(p, q)], out[:, q * C2:(q + 1) * C2])
     start(UP2, cat2)
-    over_level2(near, add, cat2, vd2a, 0, C2)
+    near_sums(True, cat2, vd2a, 0, C2)
     finish(UP2, cat2)
-    over_level2(far, done(bd2a, lambda a, b, value: put_planes(e2a, [(a, b)], value)), cat2, vd2a, 0, C2)
+    far_sums(done(bd2a, lambda a, b, value: put_planes(e2a, [(a, b)], value)), cat2, vd2a, 0, C2)
     copies[-1].wait()
 
     def put_d2(a, b, value):
@@ -499,12 +514,14 @@
          w_up1, w_dec1a, b_dec1a, w_dec1b, b_dec1b, w_head, b_head) = params
         anywhere = pl.BlockSpec(memory_space=pl.ANY)
         vmem = pl.BlockSpec(memory_space=pltpu.VMEM)
+        small = [
+            jnp.transpose(image_tile, (2, 0, 1)), w_enc1a, w_head.T, b_enc1a, b_enc1b, b_enc2a, b_enc2b,
+            b_mid_a, b_mid_b, b_dec2a, b_dec2b, b_dec1a, b_dec1b,
+        ]
         operands = [
-            jnp.transpose(image_tile, (2, 0, 1)), w_enc1a, w_enc1b, w_enc2a, w_enc2b, w_mid_a, w_mid_b,
-            w_up2, w_dec2a, w_dec2b, jnp.swapaxes(w_up1, 2, 3), jnp.swapaxes(w_dec1a, 2, 3), w_dec1b, w_head.T,
-            b_enc1a, b_enc1b, b_enc2a, b_enc2b, b_mid_a, b_mid_b, b_dec2a, b_dec2b, b_dec1a, b_dec1b,
+            w_enc1b, w_enc2a, w_enc2b, w_mid_a, w_mid_b, w_up2, w_dec2a, w_dec2b,
+            jnp.swapaxes(w_up1, 2, 3), jnp.swapaxes(w_dec1a, 2, 3), w_dec1b,
         ]
-        specs = [vmem] * 2 + [anywhere] * 11 + [vmem] * 11
 
         def kept(*shape, dtype=BF16):
             return pltpu.VMEM(shape, dtype)
@@ -524,16 +541,17 @@
         scratch += [kept(factor, SIDE, width) for factor, width in EXCHANGE]
         scratch += [kept(factor + 2, SIDE, width) for factor, width in EXCHANGE]
         links = pltpu.SemaphoreType.DMA((len(EXCHANGE), MESSAGES))
-        scratch += [pltpu.SemaphoreType.DMA((LOADS,)), links, links]
+        scratch += [pltpu.SemaphoreType.DMA((LOADS,)), links, links, pltpu.SemaphoreType.DMA((SMALL,))]
+        scratch = [kept(*array.shape, dtype=array.dtype) for array in small] + scratch
         out = pl.pallas_call(
             functools.partial(kernel, mesh.shape["row"]),
             name="unet",
             out_shape=jax.ShapeDtypeStruct((6, HALF, HALF), F32),
-            in_specs=specs,
+            in_specs=[anywhere] * (len(operands) + SMALL),
             out_specs=vmem,
             scratch_shapes=scratch,
             compiler_params=pltpu.CompilerParams(collective_id=0, has_side_effects=True, vmem_limit_bytes=67043328),
-        )(*operands)
+        )(*operands, *small)
         return jnp.transpose(out, (1, 2, 0)) + b_head
 
     def program(image, *params):

time: 74.3 us -> 71.3 us (0.960)
  Pallas kernels: 72.4 us -> 69.5 us
    pallas_call x1, Pallas kernels: 72.4 us -> 69.5 us  [device_body(): pl.pallas_call(functools.partial(kernel, mesh.shape['row']), name='unet',...]
where the time goes in v4:
time: 71.3 us; the launch traced here: 71.2 us
  Pallas kernels  69.5 us (97%)
  other arithmetic  1.69 us (2%)
    pallas_call x1, Pallas kernels, device_body(): pl.pallas_call(functools.partial(kernel, mesh.shape['row']), name='unet',...  69.5 us
    add x1, other arithmetic, device_body(): return jnp.transpose(out, (1, 2, 0)) + b_head  1.69 us

profile of v4, /device:TPU:0, one launch (start us, length us, event | category | flops | bytes accessed | tf_op | source)
XLA Modules:
  0.0 71.2 jit_solution(17975231160993615658)
XLA Ops:
  0.0 69.5 %unet.1 = f32[6,64,64]{2,1,0:T(8,128)} custom-call(bf16[3,3,192,192]{3,2,1,0:T(8,128)(2,1)} %we1b.1, bf16[3,3,192,384]{3,2,1,0:T(8,128)(2,1)} %we2a.1, bf16[3,3,384,384]{3,2,1,0:T(8,128)(2,1)} %we2b.1, bf16[3,3,384,768]{3,2,1,0:T(8,128)(2,1)} %wma.1, bf16[3,3,768,768]{3,2,1,0:T(8,128)(2,1)} %wmb.1, bf16[2,2,768,384]{3,2,1,0:T(8,128)(2,1)} %wu2.1, ...), custom_call_target="tpu_custom_call" | custom-call | tf_op jit(solution)/shard_map/unet/pallas_call | solution.py:546
  69.5 1.7 %add_bitcast_fusion = f32[64,64,6]{1,0,2:T(8,128)} fusion(f32[6,64,64]{2,1,0:T(8,128)} %unet.1, f32[6]{0:T(128)} %param.49), kind=kLoop, calls=%fused_computation | loop fusion | flops 24576 | bytes 196632 | tf_op jit(solution)/shard_map/add | solution.py:555

commit v5 on v4

--- a/solution.py
+++ b/solution.py
@@ -387,10 +387,8 @@
     def _():
         h1[0, :, ROWS - 1] = jnp.zeros((6, SIDE, C1P), BF16)
 
-    @pl.loop(0, 2)
-    def _(t):
-        for a in (2 * t, 2 * t + 1):
-            put_planes(cat1, row_of(a), biased_relu(conv(h1, 4, row_of(a), ve1b), bpad.at[1:2, :C1P]), LANE)
+    for a in range(4):
+        put_planes(cat1, row_of(a), biased_relu(conv(h1, 4, row_of(a), ve1b), bpad.at[1:2, :C1P]), LANE)
 
     pool(cat1, p1, 2, LANE, C1P)
 
@@ -456,8 +454,7 @@
     conv_level2(DEC2A, e2a, ve2b, bd2b, put_d2)
     copies[7].wait()
 
-    @pl.loop(0, 2)
-    def _(t):
+    for t in range(2):
         lhs = d2[pl.ds(2 * t * PIX, 2 * PIX)]
         for p, q in LEVEL2:
             put_planes(cat1, [(2 * t + p, q), (2 * t + p, q + 2)], dot_rows(lhs, vu1[p, q]).astype(BF16))
@@ -467,19 +464,20 @@
 
     border = 3 * col
 
-    def level1(index, src, layer):
-        start(index, src)
-        for a in (1, 2):
-            layer([(a, 1), (a, 2), (a, border)])
-        finish(index, src)
-        layer([(1, 3 - border), (2, 3 - border)])
-        for a in (0, 3):
-            layer(row_of(a))
-
     def dec1a(planes):
         put_planes(d1a, planes, biased_relu(dot_rows(gather(cat1, 4, planes), vd1a[...]), bpad.at[2:3, :C1P]))
 
-    level1(CAT1, cat1, dec1a)
+    inner = (1, 2)
+    fixed = [(a, 3 - border) for a in inner]
+    start(CAT1, cat1)
+    dec1a([(1, b) for b in inner])
+    dec1a([(a, border) for a in inner])
+    finish(CAT1, cat1)
+    dec1a(fixed)
+    for a in (0, 3):
+        dec1a(row_of(a))
+    start(DEC1A, d1a)
+    dec1a([(2, b) for b in inner])
     copies[17].wait()
 
     def head(a):
@@ -489,8 +487,14 @@
     def dec1b(planes):
         put_planes(h1, planes, biased_relu(conv(d1a, 4, planes, vd1b), bd1b))
 
-    level1(DEC1A, d1a, dec1b)
-    for a in range(4):
+    for a in inner:
+        dec1b([(a, b) for b in (*inner, border)])
+    finish(DEC1A, d1a)
+    dec1b(fixed)
+    for a in inner:
+        head(a)
+    for a in (0, 3):
+        dec1b(row_of(a))
         head(a)
     wide = 2 * PIX
     flat = jnp.concatenate([heads[a, :, h * wide:(h + 1) * wide] for a in range(4) for h in range(2)], axis=0)

time: 71.3 us -> 74.9 us (1.050)
  Pallas kernels: 69.5 us -> 73.1 us
    pallas_call x1, Pallas kernels: 69.5 us -> 73.1 us  [device_body(): pl.pallas_call(functools.partial(kernel, mesh.shape['row']), name='unet',...]
where the time goes in v5:
time: 74.9 us; the launch traced here: 74.8 us
  Pallas kernels  73.1 us (98%)
  other arithmetic  1.69 us (2%)
    pallas_call x1, Pallas kernels, device_body(): pl.pallas_call(functools.partial(kernel, mesh.shape['row']), name='unet',...  73.1 us
    add x1, other arithmetic, device_body(): return jnp.transpose(out, (1, 2, 0)) + b_head  1.69 us

profile of v5, /device:TPU:0, one launch (start us, length us, event | category | flops | bytes accessed | tf_op | source)
XLA Modules:
  0.0 74.8 jit_solution(13178767573981925511)
XLA Ops:
  0.0 73.1 %unet.1 = f32[6,64,64]{2,1,0:T(8,128)} custom-call(bf16[3,3,192,192]{3,2,1,0:T(8,128)(2,1)} %we1b.1, bf16[3,3,192,384]{3,2,1,0:T(8,128)(2,1)} %we2a.1, bf16[3,3,384,384]{3,2,1,0:T(8,128)(2,1)} %we2b.1, bf16[3,3,384,768]{3,2,1,0:T(8,128)(2,1)} %wma.1, bf16[3,3,768,768]{3,2,1,0:T(8,128)(2,1)} %wmb.1, bf16[2,2,768,384]{3,2,1,0:T(8,128)(2,1)} %wu2.1, ...), custom_call_target="tpu_custom_call" | custom-call | tf_op jit(solution)/shard_map/unet/pallas_call | solution.py:550
  73.1 1.7 %add_bitcast_fusion = f32[64,64,6]{1,0,2:T(8,128)} fusion(f32[6,64,64]{2,1,0:T(8,128)} %unet.1, f32[6]{0:T(128)} %param.49), kind=kLoop, calls=%fused_computation | loop fusion | flops 24576 | bytes 196632 | tf_op jit(solution)/shard_map/add | solution.py:559

commit v6 on v5

--- a/solution.py
+++ b/solution.py
@@ -387,8 +387,10 @@
     def _():
         h1[0, :, ROWS - 1] = jnp.zeros((6, SIDE, C1P), BF16)
 
-    for a in range(4):
-        put_planes(cat1, row_of(a), biased_relu(conv(h1, 4, row_of(a), ve1b), bpad.at[1:2, :C1P]), LANE)
+    @pl.loop(0, 2)
+    def _(t):
+        for a in (2 * t, 2 * t + 1):
+            put_planes(cat1, row_of(a), biased_relu(conv(h1, 4, row_of(a), ve1b), bpad.at[1:2, :C1P]), LANE)
 
     pool(cat1, p1, 2, LANE, C1P)
 
@@ -454,7 +456,8 @@
     conv_level2(DEC2A, e2a, ve2b, bd2b, put_d2)
     copies[7].wait()
 
-    for t in range(2):
+    @pl.loop(0, 2)
+    def _(t):
         lhs = d2[pl.ds(2 * t * PIX, 2 * PIX)]
         for p, q in LEVEL2:
             put_planes(cat1, [(2 * t + p, q), (2 * t + p, q + 2)], dot_rows(lhs, vu1[p, q]).astype(BF16))
@@ -491,10 +494,9 @@
         dec1b([(a, b) for b in (*inner, border)])
     finish(DEC1A, d1a)
     dec1b(fixed)
-    for a in inner:
-        head(a)
     for a in (0, 3):
         dec1b(row_of(a))
+    for a in range(4):
         head(a)
     wide = 2 * PIX
     flat = jnp.concatenate([heads[a, :, h * wide:(h + 1) * wide] for a in range(4) for h in range(2)], axis=0)

time: 74.9 us -> 72 us (0.961)
  Pallas kernels: 73.1 us -> 70.2 us
    pallas_call x1, Pallas kernels: 73.1 us -> 70.2 us  [device_body(): pl.pallas_call(functools.partial(kernel, mesh.shape['row']), name='unet',...]
where the time goes in v6:
time: 72 us; the launch traced here: 71.9 us
  Pallas kernels  70.2 us (98%)
  other arithmetic  1.69 us (2%)
    pallas_call x1, Pallas kernels, device_body(): pl.pallas_call(functools.partial(kernel, mesh.shape['row']), name='unet',...  70.2 us
    add x1, other arithmetic, device_body(): return jnp.transpose(out, (1, 2, 0)) + b_head  1.69 us

profile of v6, /device:TPU:0, one launch (start us, length us, event | category | flops | bytes accessed | tf_op | source)
XLA Modules:
  0.0 71.9 jit_solution(18141000442772892946)
XLA Ops:
  0.0 70.2 %unet.1 = f32[6,64,64]{2,1,0:T(8,128)} custom-call(bf16[3,3,192,192]{3,2,1,0:T(8,128)(2,1)} %we1b.1, bf16[3,3,192,384]{3,2,1,0:T(8,128)(2,1)} %we2a.1, bf16[3,3,384,384]{3,2,1,0:T(8,128)(2,1)} %we2b.1, bf16[3,3,384,768]{3,2,1,0:T(8,128)(2,1)} %wma.1, bf16[3,3,768,768]{3,2,1,0:T(8,128)(2,1)} %wmb.1, bf16[2,2,768,384]{3,2,1,0:T(8,128)(2,1)} %wu2.1, ...), custom_call_target="tpu_custom_call" | custom-call | tf_op jit(solution)/shard_map/unet/pallas_call | solution.py:552
  70.2 1.7 %add_bitcast_fusion = f32[64,64,6]{1,0,2:T(8,128)} fusion(f32[6,64,64]{2,1,0:T(8,128)} %unet.1, f32[6]{0:T(128)} %param.49), kind=kLoop, calls=%fused_computation | loop fusion | flops 24576 | bytes 196632 | tf_op jit(solution)/shard_map/add | solution.py:561

commit v7 on v4

--- a/solution.py
+++ b/solution.py
@@ -420,9 +420,8 @@
     finish(POOL2, p2)
 
     def conv_level3(src, weight, bias, put):
-        @pl.loop(0, 3)
-        def _(n):
-            lanes = pl.ds(pl.multiple_of(n * PIX, PIX), PIX)
+        for n in range(3):
+            lanes = pl.ds(n * PIX, PIX)
             flat = weight[:, :, :, lanes].reshape(9 * src.shape[-1], PIX)
             put(lanes, biased_relu(dot(gather(src, 1, [(0, 0)]), flat), bpad.at[bias:bias + 1, lanes]))
 

time: 71.3 us -> 72 us (level)
    pallas_call x1, Pallas kernels: 69.5 us -> 70.2 us  [device_body(): pl.pallas_call(functools.partial(kernel, mesh.shape['row']), name='unet',...]
where the time goes in v7:
time: 72 us; the launch traced here: 71.9 us
  Pallas kernels  70.2 us (98%)
  other arithmetic  1.69 us (2%)
    pallas_call x1, Pallas kernels, device_body(): pl.pallas_call(functools.partial(kernel, mesh.shape['row']), name='unet',...  70.2 us
    add x1, other arithmetic, device_body(): return jnp.transpose(out, (1, 2, 0)) + b_head  1.69 us

profile of v7, /device:TPU:0, one launch (start us, length us, event | category | flops | bytes accessed | tf_op | source)
XLA Modules:
  0.0 71.9 jit_solution(17577925590616529288)
XLA Ops:
  0.0 70.2 %unet.1 = f32[6,64,64]{2,1,0:T(8,128)} custom-call(bf16[3,3,192,192]{3,2,1,0:T(8,128)(2,1)} %we1b.1, bf16[3,3,192,384]{3,2,1,0:T(8,128)(2,1)} %we2a.1, bf16[3,3,384,384]{3,2,1,0:T(8,128)(2,1)} %we2b.1, bf16[3,3,384,768]{3,2,1,0:T(8,128)(2,1)} %wma.1, bf16[3,3,768,768]{3,2,1,0:T(8,128)(2,1)} %wmb.1, bf16[2,2,768,384]{3,2,1,0:T(8,128)(2,1)} %wu2.1, ...), custom_call_target="tpu_custom_call" | custom-call | tf_op jit(solution)/shard_map/unet/pallas_call | solution.py:545
  70.2 1.7 %add_bitcast_fusion = f32[64,64,6]{1,0,2:T(8,128)} fusion(f32[6,64,64]{2,1,0:T(8,128)} %unet.1, f32[6]{0:T(128)} %param.49), kind=kLoop, calls=%fused_computation | loop fusion | flops 24576 | bytes 196632 | tf_op jit(solution)/shard_map/add | solution.py:554
